TPU v7x, 32 devices: a whole 2x2x4 slice. The times are simulated.
32 devices in a mesh: fsdp: 4 (over y, core), tp: 4 (over z), rollout: 2 (over x).
Axes of the slice: x: 2, y: 2, z: 4, core: 2. Of those that a mesh axis runs over, the one named last changes fastest.
Arguments:
- weights: bfloat16 [2, 4096, 14336], P('rollout', 'fsdp', 'tp'), may hold values from -6 to 6
- gradient: bfloat16 [2, 4096, 14336], P('rollout', 'fsdp', 'tp'), may hold values from -6 to 6
- momentum: float32 [2, 4096, 14336], P('rollout', 'fsdp', 'tp'), may hold values from -90 to 90
- basis: float32 [2, 14336, 512], P('rollout', 'tp'), may hold values from -6 to 6
Outputs:
- weights_next: bfloat16 [2, 4096, 14336], P('rollout', 'fsdp', 'tp')
- momentum_next: float32 [2, 4096, 14336], P('rollout', 'fsdp', 'tp')
- basis_next: float32 [2, 14336, 512], P('rollout', 'tp')
- rollout_weights: bfloat16 [2, 4096, 14336], P(None, 'fsdp', 'tp')
All inputs are finite; a program needn't handle non-finite values.
Results may differ from a plain program's by a relative error of at most 0.013.
Values may be sent and summed in bfloat16 or wider, within the bound.
A program may use at most 192 MiB of HBM per device.

v0:
```python
import jax
import jax.numpy as jnp
from jax import lax
from jax.sharding import PartitionSpec as P

COLS = 14336
HIGH = lax.Precision.HIGHEST


def body(weights, gradient, momentum, basis):
    blend = momentum[0] + gradient[0].astype(jnp.float32)
    prior = basis[0]
    share = lax.psum_scatter(
        jnp.dot(blend, prior, precision=HIGH, preferred_element_type=jnp.float32),
        "tp",
        scatter_dimension=0,
        tiled=True,
    )
    gram = lax.psum(
        jnp.dot(share.T, share, precision=HIGH, preferred_element_type=jnp.float32), ("fsdp", "tp")
    )
    left = lax.all_gather(share, "tp", axis=0, tiled=True)
    lower = jnp.linalg.cholesky(gram)
    ortho = lax.linalg.triangular_solve(lower, left, left_side=False, lower=True, transpose_a=True)
    partial_right = jnp.dot(blend.T, ortho, precision=HIGH, preferred_element_type=jnp.float32)
    right = lax.psum(partial_right.astype(jnp.bfloat16), "fsdp").astype(jnp.float32)
    squares = lax.psum(jnp.sum(right * right, axis=0), "tp")
    meansq = squares / COLS
    basis_new = right * lax.rsqrt(meansq + 1e-06)
    norms = jnp.sqrt(meansq + 1e-06)
    moment_new = blend - 0.05 * jnp.dot(
        ortho * norms, basis_new.T, precision=HIGH, preferred_element_type=jnp.float32
    )
    update = jnp.dot(ortho, basis_new.T, precision=HIGH, preferred_element_type=jnp.float32)
    weight_new = (weights[0].astype(jnp.float32) - 0.3 * update).astype(jnp.bfloat16)[None]
    rollout_copy = lax.all_gather(weight_new, "rollout", axis=0, tiled=True)
    return (weight_new, moment_new[None], basis_new[None], rollout_copy)


def solution(mesh):
    return jax.shard_map(
        body,
        mesh=mesh,
        in_specs=(
            P("rollout", "fsdp", "tp"),
            P("rollout", "fsdp", "tp"),
            P("rollout", "fsdp", "tp"),
            P("rollout", "tp", None),
        ),
        out_specs=(
            P("rollout", "fsdp", "tp"),
            P("rollout", "fsdp", "tp"),
            P("rollout", "tp", None),
            P(None, "fsdp", "tp"),
        ),
        check_vma=False,
    )
```

profile of v0, /device:TPU:0, one launch (start us, length us, event | category | flops | bytes accessed | tf_op | source)
XLA Modules:
  0.0 710.0 jit_solution(7459058599054322177)
XLA Ops:
  7.2 29.3 %fusion.3 = f32[1024,512]{1,0:T(8,128)} fusion(f32[1,3584,512]{2,1,0:T(8,128)} %param.7, f32[1,1024,3584]{2,1,0:T(8,128)} %param.6, bf16[1,1024,3584]{2,1,0:T(8,128)(2,1)} %param.5), kind=kOutput, calls=%fused_computation.7 | convolution fusion | flops 22555918336 | bytes 31457280 | tf_op jit(solution)/shard_map/dot_general | solution.py:14
  36.5 46.5 %reduce-scatter.2.cloned.1.call-done = f32[256,512]{1,0:T(8,128)} async-done(((f32[1024,512]{1,0:T(8,128)}), f32[256,512]{1,0:T(8,128)}) %reduce-scatter.2.cloned.1.call-update) | async-done | bytes 524304 | tf_op jit(solution)/shard_map/reduce_scatter | solution.py:13
  83.0 3.2 fusion.58
  86.3 0.7 all-gather.4.cloned.1.call-update
  87.0 0.5 all-reduce.6.cloned.1.call-start
  87.5 92.5 %all-reduce.4.cloned.1.call-done = f32[512,512]{0,1:T(8,128)} async-done(((f32[512,512]{0,1:T(8,128)}), f32[512,512]{0,1:T(8,128)}) %all-reduce.4.cloned.1.call-update) | async-done | bytes 1048592 | tf_op jit(solution)/shard_map/psum | solution.py:19
  180.0 1.6 copy.9
  181.6 1.4 fusion.29
  183.1 11.7 %cholesky.104 = f32[128,128]{1,0:T(8,128)S(1)} custom-call(f32[128,128]{1,0:T(8,128)S(1)} %cholesky.266), custom_call_target="Cholesky" | custom-call | tf_op jit(solution)/shard_map/jit(cholesky)/cholesky | solution.py:23
  194.8 9.8 %custom-call.30 = f32[1,128,128]{1,2,0:T(8,128)S(1)} custom-call(f32[1,128,128]{2,1,0:T(8,128)S(1)} %get-tuple-element.31), custom_call_target="InvertDiagBlocksLowerTriangular" | custom-call | tf_op jit(solution)/shard_map/jit(cholesky)/cholesky | solution.py:23
  204.8 0.3 constant_dynamic-update-slice_fusion.3
  205.1 0.3 convolution_subtract_fusion.2
  205.4 11.7 %cholesky.217 = f32[128,128]{1,0:T(8,128)S(1)} custom-call(f32[128,128]{1,0:T(8,128)S(1)} %cholesky.270), custom_call_target="Cholesky" | custom-call | tf_op jit(solution)/shard_map/jit(cholesky)/cholesky | solution.py:23
  217.2 10.0 %custom-call.31 = f32[1,128,128]{1,2,0:T(8,128)S(1)} custom-call(f32[1,128,128]{2,1,0:T(8,128)S(1)} %get-tuple-element.28), custom_call_target="InvertDiagBlocksLowerTriangular" | custom-call | tf_op jit(solution)/shard_map/jit(cholesky)/cholesky | solution.py:23
  227.4 0.4 convolution_subtract_fusion.3
  227.8 11.7 %cholesky.238 = f32[128,128]{1,0:T(8,128)S(1)} custom-call(f32[128,128]{1,0:T(8,128)S(1)} %cholesky.275), custom_call_target="Cholesky" | custom-call | tf_op jit(solution)/shard_map/jit(cholesky)/cholesky | solution.py:23
  239.6 9.8 %custom-call.32 = f32[1,128,128]{1,2,0:T(8,128)S(1)} custom-call(f32[1,128,128]{2,1,0:T(8,128)S(1)} %get-tuple-element.25), custom_call_target="InvertDiagBlocksLowerTriangular" | custom-call | tf_op jit(solution)/shard_map/jit(cholesky)/cholesky | solution.py:23
  249.6 0.4 convolution_subtract_fusion.4
  250.0 11.7 %cholesky.255 = f32[128,128]{1,0:T(8,128)S(1)} custom-call(f32[128,128]{1,0:T(8,128)S(1)} %convolution_subtract_fusion.4), custom_call_target="Cholesky" | custom-call | tf_op jit(solution)/shard_map/jit(cholesky)/cholesky | solution.py:23
  261.7 0.6 compare_reduce_fusion.2
  263.6 0.6 compare_reduce_fusion.1
  265.0 0.6 compare_reduce_fusion
  266.6 8.0 %while.1 = (s32[]{:T(128)}, f32[512,512]{1,0:T(8,128)S(1)}, s32[4,2]{0,1:T(2,128)S(1)}, f32[4,128,128]{2,1,0:T(8,128)S(1)}, s32[]{:T(128)}) while((s32[]{:T(128)}, f32[512,512]{1,0:T(8,128)S(1)}, s32[4,2]{0,1:T(2,128)S(1)}, f32[4,128,128]{2,1,0:T(8,128)S(1)}, s32[]{:T(128)}) %tuple.32), condition=%wide.while_cond, body=%wide.while_body.sunk | while | flops 2 | bytes 131189 | solution.py:24
  266.7 0.5 fusion.67
  267.2 1.4 bitcast_dynamic-update-slice_fusion.2
  268.7 0.5 fusion.67
  269.2 1.4 bitcast_dynamic-update-slice_fusion.2
  270.7 0.5 fusion.67
  271.2 1.4 bitcast_dynamic-update-slice_fusion.2
  272.7 0.5 fusion.67
  273.2 1.4 bitcast_dynamic-update-slice_fusion.2
  274.6 39.3 %custom-call.33 = f32[4,128,128]{1,2,0:T(8,128)S(1)} custom-call(f32[4,128,128]{2,1,0:T(8,128)S(1)} %get-tuple-element.11), custom_call_target="InvertDiagBlocksLowerTriangular" | custom-call | tf_op jit(solution)/shard_map/triangular_solve | solution.py:24
  314.0 1.7 fusion.31
  315.6 2.0 convolution_subtract_fusion.1
  317.7 0.6 fusion.43
  318.3 2.9 convolution_subtract_fusion
  321.2 0.6 fusion.42
  321.8 3.7 fusion.23
  325.5 0.6 fusion.41
  326.1 50.1 %fusion.11 = bf16[3584,512]{1,0:T(8,128)(2,1)} fusion(f32[1,1024,3584]{2,1,0:T(8,128)} %param.6, bf16[1,1024,3584]{2,1,0:T(8,128)(2,1)} %param.5, f32[1024,128]{0,1:T(8,128)S(1)} %fusion.41, f32[1024,128]{0,1:T(8,128)S(1)} %fusion.42, f32[1024,128]{0,1:T(8,128)S(1)} %fusion.43, f32[1024,128]{0,1:T(8,128)S(1)} %fusion.31), kind=kOutput, calls=%fused_computation.18 | convolution fusion | flops 22559326208 | bytes 27787264 | tf_op jit(solution)/shard_map/dot_general | solution.py:25
  376.3 76.2 %all-reduce.6.cloned.1.call-done = bf16[3584,512]{1,0:T(8,128)(2,1)} async-done(((bf16[3584,512]{1,0:T(8,128)(2,1)}), bf16[3584,512]{1,0:T(8,128)(2,1)}) %all-reduce.6.cloned.1.call-update) | async-done | bytes 3670032 | tf_op jit(solution)/shard_map/psum | solution.py:26
  452.5 2.9 fusion.9
  455.3 11.9 %psum.23 = f32[512]{0:T(512)S(1)} all-reduce(f32[512]{0:T(512)S(1)} %fusion.9), channel_id=1, replica_groups=mesh['fsdp'=4,'tp'=4,'rollout'=2] {'tp'}, use_global_device_ids=true, to_apply=%region_12.13 | all-reduce | flops 512 | bytes 4096 | tf_op jit(solution)/shard_map/psum | solution.py:27
  467.2 49.9 %fusion = bf16[1024,3584]{1,0:T(8,128)(2,1)} fusion(bf16[1,1024,3584]{2,1,0:T(8,128)(2,1)} %param.4, bf16[3584,512]{1,0:T(8,128)(2,1)} %all-reduce.6.cloned.1.call-done, f32[512]{0:T(512)S(1)} %get-tuple-element.33, f32[1024,128]{0,1:T(8,128)S(1)} %fusion.41, f32[1024,128]{0,1:T(8,128)S(1)} %fusion.42, f32[1024,128]{0,1:T(8,128)S(1)} %fusion.43, ...), kind=kOutput, calls=%fused_computation.3 | convolution fusion | flops 22568501248 | bytes 20449280 | tf_op jit(solution)/shard_map/dot_general | solution.py:34
  517.1 7.9 %fusion.6 = f32[1,3584,512]{2,1,0:T(8,128)} fusion(bf16[3584,512]{1,0:T(8,128)(2,1)} %all-reduce.6.cloned.1.call-done, f32[512]{0:T(512)S(1)} %get-tuple-element.33), kind=kLoop, calls=%fused_computation.13 | loop fusion | flops 3670016 | bytes 11012096 | tf_op jit(solution)/shard_map/broadcast_in_dim | solution.py:37
  525.0 52.9 %fusion.5 = f32[1,1024,3584]{2,1,0:T(8,128)} fusion(bf16[3584,512]{1,0:T(8,128)(2,1)S(1)} %copy-done, f32[1,1024,3584]{2,1,0:T(8,128)} %param.6, bf16[1,1024,3584]{2,1,0:T(8,128)(2,1)} %param.5, f32[512]{0:T(512)S(1)} %get-tuple-element.33, f32[512]{0:T(512)S(1)} %get-tuple-element.32, f32[1024,128]{0,1:T(8,128)S(1)} %fusion.41, ...), kind=kOutput, calls=%fused_computation.9 | convolution fusion | flops 22569025536 | bytes 42471424 | tf_op jit(solution)/shard_map/dot_general | solution.py:31
  577.9 112.2 %all-gather.6.cloned.1.call-done = bf16[2048,3584]{1,0:T(8,128)(2,1)} async-done(((bf16[1024,3584]{1,0:T(8,128)(2,1)}), bf16[2048,3584]{1,0:T(8,128)(2,1)}) %all-gather.6.cloned.1.call-update) | async-done | bytes 14680080 | tf_op jit(solution)/shard_map/all_gather | solution.py:36
  690.1 13.1 %copy.29 = bf16[2,1024,3584]{2,1,0:T(8,128)(2,1)} copy(bf16[2,1024,3584]{2,1,0:T(8,128)(2,1)} %bitcast.72) | data formatting | bytes 29360128
  (30 shorter events, 1.7 us)
Async XLA Ops:
  7.2 75.8 %reduce-scatter.2.cloned.1.call-start = ((), (), s32[]{:S(2)}) async-start(), calls=%async_computation.1 | async-start | bytes 2621440 | tf_op jit(solution)/shard_map/reduce_scatter | solution.py:13
  36.5 143.6 %all-reduce.4.cloned.1.call-start = ((), (), s32[]{:S(2)}) async-start(), calls=%async_computation.3 | async-start | bytes 2097152 | tf_op jit(solution)/shard_map/psum | solution.py:19
  86.2 227.7 %all-gather.4.cloned.1.call-start = ((), (), s32[]{:S(2)}) async-start(), calls=%async_computation.2 | async-start | bytes 2621440 | tf_op jit(solution)/shard_map/all_gather | solution.py:22
  87.0 365.5 %all-reduce.6.cloned.1.call-start = ((), (), s32[]{:S(2)}) async-start(), calls=%async_computation.4 | async-start | bytes 7340032 | tf_op jit(solution)/shard_map/psum | solution.py:26
  376.2 313.9 %all-gather.6.cloned.1.call-start = ((), (), s32[]{:S(2)}) async-start(), calls=%async_computation.5 | async-start | bytes 22020096 | tf_op jit(solution)/shard_map/all_gather | solution.py:36
  517.1 7.9 %copy-start = (bf16[3584,512]{1,0:T(8,128)(2,1)S(1)}, bf16[3584,512]{1,0:T(8,128)(2,1)}, u32[]{:S(2)}) copy-start(bf16[3584,512]{1,0:T(8,128)(2,1)} %all-reduce.6.cloned.1.call-done) | copy-start | bytes 11010052
Sparse Core Ops, SparseCore 0:
  36.6 46.3 reduce-scatter.1
  87.0 92.9 all-reduce.3
  181.6 44.7 all-gather.3
  376.4 76.0 all-reduce.5
  517.2 172.8 all-gather.5
where the time goes:
time: 716 us; the launch traced here: 710 us
  waiting for transfers between devices  328 us (46%)
  matrix products  199 us (28%)
  other arithmetic  130 us (18%)
  local copies, waits for them, and re-layouts  22.9 us (3%)
  between operations  16.8 us (2%)
  blocking collectives  11.9 us (2%)
    all_gather x1, waiting for transfers between devices, body(): rollout_copy = lax.all_gather(weight_new, 'rollout', axis=0, tiled=True)  112 us
    psum x1, waiting for transfers between devices, body(): lax.psum(jnp.dot(share.T, share, precision=HIGH, preferred_element_type=j...  92.5 us
    another operation x14, other arithmetic, body(): lower = jnp.linalg.cholesky(gram)  78.5 us
    psum x1, waiting for transfers between devices, body(): lax.psum(partial_right.astype(jnp.bfloat16), 'fsdp').astype(jnp.float32)  76.2 us
    dot_general x1, matrix products, body(): jnp.dot(ortho * norms, basis_new.T, precision=HIGH, preferred_element_typ...  52.9 us
    dot_general x1, matrix products, body(): jnp.dot(blend.T, ortho, precision=HIGH, preferred_element_type=jnp.float32)  50.1 us
    dot_general x1, matrix products, body(): jnp.dot(ortho, basis_new.T, precision=HIGH, preferred_element_type=jnp.fl...  49.9 us
    reduce_scatter x1, waiting for transfers between devices, body(): lax.psum_scatter(jnp.dot(blend, prior, precision=HIGH, preferred_element_...  46.5 us
  transfers between devices with their start and end apart: 5, of which 4 were waited for; matrix products, arithmetic and copies ran while one was open for 27% of the time, Pallas kernels for 0%

commit v1 on v0

--- a/solution.py
+++ b/solution.py
@@ -16,8 +16,12 @@
         scatter_dimension=0,
         tiled=True,
     )
-    gram = lax.psum(
-        jnp.dot(share.T, share, precision=HIGH, preferred_element_type=jnp.float32), ("fsdp", "tp")
+    gram = jnp.sum(
+        lax.all_gather(
+            jnp.dot(share.T, share, precision=HIGH, preferred_element_type=jnp.float32),
+            ("fsdp", "tp"),
+        ),
+        axis=0,
     )
     left = lax.all_gather(share, "tp", axis=0, tiled=True)
     lower = jnp.linalg.cholesky(gram)

time: 716 us -> 752 us (1.050)
  waiting for transfers between devices: 328 us -> 359 us
    all_gather x0 -> x1, waiting for transfers between devices: none -> 125 us  [body(): lax.all_gather(jnp.dot(share.T, share, precision=HIGH, preferred_element_...]
    psum x1 -> x0, waiting for transfers between devices: 92.5 us -> none  [body(): lax.psum(jnp.dot(share.T, share, precision=HIGH, preferred_element_type=j...]
    reduce_sum x0 -> x1, other arithmetic: none -> 7.91 us  [body(): jnp.sum(lax.all_gather(jnp.dot(share.T, share, precision=HIGH, preferred_...]
  transfers between devices with their start and end apart: 5 -> 5, of which waited for: 4 -> 4; matrix products, arithmetic and copies ran while one was open for 27% -> 26% of each run, Pallas kernels for 0% -> 0%
where the time goes in v1:
time: 752 us; the launch traced here: 747 us
  waiting for transfers between devices  359 us (48%)
  matrix products  199 us (26%)
  other arithmetic  137 us (18%)
  local copies, waits for them, and re-layouts  21.5 us (3%)
  between operations  16.8 us (2%)
  blocking collectives  11.9 us (2%)
    all_gather x1, waiting for transfers between devices, body(): lax.all_gather(jnp.dot(share.T, share, precision=HIGH, preferred_element_...  125 us
    all_gather x1, waiting for transfers between devices, body(): rollout_copy = lax.all_gather(weight_new, 'rollout', axis=0, tiled=True)  112 us
    another operation x14, other arithmetic, body(): lower = jnp.linalg.cholesky(gram)  78.9 us
    psum x1, waiting for transfers between devices, body(): lax.psum(partial_right.astype(jnp.bfloat16), 'fsdp').astype(jnp.float32)  75.2 us
    dot_general x1, matrix products, body(): jnp.dot(ortho * norms, basis_new.T, precision=HIGH, preferred_element_typ...  52.9 us
    dot_general x1, matrix products, body(): jnp.dot(blend.T, ortho, precision=HIGH, preferred_element_type=jnp.float32)  50.1 us
    dot_general x1, matrix products, body(): jnp.dot(ortho, basis_new.T, precision=HIGH, preferred_element_type=jnp.fl...  49.9 us
    reduce_scatter x1, waiting for transfers between devices, body(): lax.psum_scatter(jnp.dot(blend, prior, precision=HIGH, preferred_element_...  46.5 us
  transfers between devices with their start and end apart: 5, of which 4 were waited for; matrix products, arithmetic and copies ran while one was open for 26% of the time, Pallas kernels for 0%

profile of v1, /device:TPU:0, one launch (start us, length us, event | category | flops | bytes accessed | tf_op | source)
XLA Modules:
  0.0 746.7 jit_solution(12389121948933850193)
XLA Ops:
  7.2 29.3 %fusion.3 = f32[1024,512]{1,0:T(8,128)} fusion(f32[1,3584,512]{2,1,0:T(8,128)} %param.7, f32[1,1024,3584]{2,1,0:T(8,128)} %param.6, bf16[1,1024,3584]{2,1,0:T(8,128)(2,1)} %param.5), kind=kOutput, calls=%fused_computation.7 | convolution fusion | flops 22555918336 | bytes 31457280 | tf_op jit(solution)/shard_map/dot_general | solution.py:14
  36.5 46.5 %reduce-scatter.2.cloned.1.call-done = f32[256,512]{1,0:T(8,128)} async-done(((f32[1024,512]{1,0:T(8,128)}), f32[256,512]{1,0:T(8,128)}) %reduce-scatter.2.cloned.1.call-update) | async-done | bytes 524304 | tf_op jit(solution)/shard_map/reduce_scatter | solution.py:13
  83.0 3.2 fusion.58
  86.3 0.7 all-gather.6.cloned.1.call-update
  87.2 124.8 %all-gather.8.cloned.1.call-done = f32[8192,512]{1,0:T(8,128)} async-done(((f32[512,512]{1,0:T(8,128)}), f32[8192,512]{1,0:T(8,128)}) %all-gather.8.cloned.1.call-update) | async-done | bytes 16777232 | tf_op jit(solution)/shard_map/all_gather | solution.py:20
  212.0 7.9 %reduce_sum.18 = f32[512,512]{1,0:T(8,128)S(1)} reduce(f32[16,512,512]{2,1,0:T(8,128)} %bitcast.73, f32[]{:T(128)} %constant.141.clone.1), dimensions={0}, to_apply=%region_1.0 | reduce | flops 3932160 | bytes 17825796 | tf_op jit(solution)/shard_map/reduce_sum | solution.py:19
  219.9 0.3 copy.9
  220.5 11.7 %cholesky.104 = f32[128,128]{1,0:T(8,128)S(1)} custom-call(f32[128,128]{1,0:T(8,128)S(1)} %cholesky.266), custom_call_target="Cholesky" | custom-call | tf_op jit(solution)/shard_map/jit(cholesky)/cholesky | solution.py:27
  232.4 9.8 %custom-call.30 = f32[1,128,128]{1,2,0:T(8,128)S(1)} custom-call(f32[1,128,128]{2,1,0:T(8,128)S(1)} %get-tuple-element.31), custom_call_target="InvertDiagBlocksLowerTriangular" | custom-call | tf_op jit(solution)/shard_map/jit(cholesky)/cholesky | solution.py:27
  242.2 0.3 constant_dynamic-update-slice_fusion.3
  242.5 0.3 convolution_subtract_fusion.2
  242.9 12.1 %cholesky.217 = f32[128,128]{1,0:T(8,128)S(1)} custom-call(f32[128,128]{1,0:T(8,128)S(1)} %cholesky.270), custom_call_target="Cholesky" | custom-call | tf_op jit(solution)/shard_map/jit(cholesky)/cholesky | solution.py:27
  255.0 9.8 %custom-call.31 = f32[1,128,128]{1,2,0:T(8,128)S(1)} custom-call(f32[1,128,128]{2,1,0:T(8,128)S(1)} %get-tuple-element.28), custom_call_target="InvertDiagBlocksLowerTriangular" | custom-call | tf_op jit(solution)/shard_map/jit(cholesky)/cholesky | solution.py:27
  264.8 0.3 convolution_dynamic-update-slice_fusion
  265.1 0.4 convolution_subtract_fusion.3
  265.5 11.7 %cholesky.238 = f32[128,128]{1,0:T(8,128)S(1)} custom-call(f32[128,128]{1,0:T(8,128)S(1)} %cholesky.275), custom_call_target="Cholesky" | custom-call | tf_op jit(solution)/shard_map/jit(cholesky)/cholesky | solution.py:27
  277.2 9.8 %custom-call.32 = f32[1,128,128]{1,2,0:T(8,128)S(1)} custom-call(f32[1,128,128]{2,1,0:T(8,128)S(1)} %get-tuple-element.25), custom_call_target="InvertDiagBlocksLowerTriangular" | custom-call | tf_op jit(solution)/shard_map/jit(cholesky)/cholesky | solution.py:27
  287.3 0.4 convolution_subtract_fusion.4
  287.7 11.9 %cholesky.255 = f32[128,128]{1,0:T(8,128)S(1)} custom-call(f32[128,128]{1,0:T(8,128)S(1)} %convolution_subtract_fusion.4), custom_call_target="Cholesky" | custom-call | tf_op jit(solution)/shard_map/jit(cholesky)/cholesky | solution.py:27
  299.5 0.6 compare_reduce_fusion.2
  301.5 0.6 compare_reduce_fusion.1
  302.8 0.6 compare_reduce_fusion
  304.2 8.0 %while.1 = (s32[]{:T(128)}, f32[512,512]{1,0:T(8,128)S(1)}, s32[4,2]{0,1:T(2,128)S(1)}, f32[4,128,128]{2,1,0:T(8,128)S(1)}, s32[]{:T(128)}) while((s32[]{:T(128)}, f32[512,512]{1,0:T(8,128)S(1)}, s32[4,2]{0,1:T(2,128)S(1)}, f32[4,128,128]{2,1,0:T(8,128)S(1)}, s32[]{:T(128)}) %tuple.32), condition=%wide.while_cond, body=%wide.while_body.sunk | while | flops 2 | bytes 131189 | solution.py:28
  304.3 0.5 fusion.67
  304.8 1.4 bitcast_dynamic-update-slice_fusion.2
  306.3 0.5 fusion.67
  306.8 1.4 bitcast_dynamic-update-slice_fusion.2
  308.3 0.5 fusion.67
  308.9 1.4 bitcast_dynamic-update-slice_fusion.2
  310.3 0.5 fusion.67
  310.9 1.4 bitcast_dynamic-update-slice_fusion.2
  312.3 39.3 %custom-call.33 = f32[4,128,128]{1,2,0:T(8,128)S(1)} custom-call(f32[4,128,128]{2,1,0:T(8,128)S(1)} %get-tuple-element.11), custom_call_target="InvertDiagBlocksLowerTriangular" | custom-call | tf_op jit(solution)/shard_map/triangular_solve | solution.py:28
  351.6 1.7 fusion.31
  353.3 2.0 convolution_subtract_fusion.1
  355.3 0.6 fusion.43
  355.9 2.9 convolution_subtract_fusion
  358.8 0.6 fusion.42
  359.4 3.7 fusion.23
  363.1 0.6 fusion.41
  363.8 50.1 %fusion.11 = bf16[3584,512]{1,0:T(8,128)(2,1)} fusion(f32[1,1024,3584]{2,1,0:T(8,128)} %param.6, bf16[1,1024,3584]{2,1,0:T(8,128)(2,1)} %param.5, f32[1024,128]{0,1:T(8,128)S(1)} %fusion.41, f32[1024,128]{0,1:T(8,128)S(1)} %fusion.42, f32[1024,128]{0,1:T(8,128)S(1)} %fusion.43, f32[1024,128]{0,1:T(8,128)S(1)} %fusion.31), kind=kOutput, calls=%fused_computation.18 | convolution fusion | flops 22559326208 | bytes 27787264 | tf_op jit(solution)/shard_map/dot_general | solution.py:29
  413.9 75.2 %all-reduce.3.cloned.1.call-done = bf16[3584,512]{1,0:T(8,128)(2,1)} async-done(((bf16[3584,512]{1,0:T(8,128)(2,1)}), bf16[3584,512]{1,0:T(8,128)(2,1)}) %all-reduce.3.cloned.1.call-update) | async-done | bytes 3670032 | tf_op jit(solution)/shard_map/psum | solution.py:30
  489.2 2.9 fusion.9
  492.1 11.9 %psum.15 = f32[512]{0:T(512)S(1)} all-reduce(f32[512]{0:T(512)S(1)} %fusion.9), channel_id=1, replica_groups=mesh['fsdp'=4,'tp'=4,'rollout'=2] {'tp'}, use_global_device_ids=true, to_apply=%region_12.13 | all-reduce | flops 512 | bytes 4096 | tf_op jit(solution)/shard_map/psum | solution.py:31
  503.9 49.9 %fusion = bf16[1024,3584]{1,0:T(8,128)(2,1)} fusion(bf16[1,1024,3584]{2,1,0:T(8,128)(2,1)} %param.4, bf16[3584,512]{1,0:T(8,128)(2,1)} %all-reduce.3.cloned.1.call-done, f32[512]{0:T(512)S(1)} %get-tuple-element.33, f32[1024,128]{0,1:T(8,128)S(1)} %fusion.41, f32[1024,128]{0,1:T(8,128)S(1)} %fusion.42, f32[1024,128]{0,1:T(8,128)S(1)} %fusion.43, ...), kind=kOutput, calls=%fused_computation.3 | convolution fusion | flops 22568501248 | bytes 20449280 | tf_op jit(solution)/shard_map/dot_general | solution.py:38
  553.8 7.9 %fusion.6 = f32[1,3584,512]{2,1,0:T(8,128)} fusion(bf16[3584,512]{1,0:T(8,128)(2,1)} %all-reduce.3.cloned.1.call-done, f32[512]{0:T(512)S(1)} %get-tuple-element.33), kind=kLoop, calls=%fused_computation.13 | loop fusion | flops 3670016 | bytes 11012096 | tf_op jit(solution)/shard_map/broadcast_in_dim | solution.py:41
  561.7 52.9 %fusion.5 = f32[1,1024,3584]{2,1,0:T(8,128)} fusion(bf16[3584,512]{1,0:T(8,128)(2,1)S(1)} %copy-done, f32[1,1024,3584]{2,1,0:T(8,128)} %param.6, bf16[1,1024,3584]{2,1,0:T(8,128)(2,1)} %param.5, f32[512]{0:T(512)S(1)} %get-tuple-element.33, f32[512]{0:T(512)S(1)} %get-tuple-element.32, f32[1024,128]{0,1:T(8,128)S(1)} %fusion.41, ...), kind=kOutput, calls=%fused_computation.9 | convolution fusion | flops 22569025536 | bytes 42471424 | tf_op jit(solution)/shard_map/dot_general | solution.py:35
  614.6 112.2 %all-gather.10.cloned.1.call-done = bf16[2048,3584]{1,0:T(8,128)(2,1)} async-done(((bf16[1024,3584]{1,0:T(8,128)(2,1)}), bf16[2048,3584]{1,0:T(8,128)(2,1)}) %all-gather.10.cloned.1.call-update) | async-done | bytes 14680080 | tf_op jit(solution)/shard_map/all_gather | solution.py:40
  726.8 13.1 %copy.27 = bf16[2,1024,3584]{2,1,0:T(8,128)(2,1)} copy(bf16[2,1024,3584]{2,1,0:T(8,128)(2,1)} %bitcast.74) | data formatting | bytes 29360128
  (31 shorter events, 1.6 us)
Async XLA Ops:
  7.2 75.8 %reduce-scatter.2.cloned.1.call-start = ((), (), s32[]{:S(2)}) async-start(), calls=%async_computation.1 | async-start | bytes 2621440 | tf_op jit(solution)/shard_map/reduce_scatter | solution.py:13
  36.5 175.5 %all-gather.8.cloned.1.call-start = ((), (), s32[]{:S(2)}) async-start(), calls=%async_computation.4 | async-start | bytes 17825792 | tf_op jit(solution)/shard_map/all_gather | solution.py:20
  86.2 265.4 %all-gather.6.cloned.1.call-start = ((), (), s32[]{:S(2)}) async-start(), calls=%async_computation.2 | async-start | bytes 2621440 | tf_op jit(solution)/shard_map/all_gather | solution.py:26
  87.0 402.2 %all-reduce.3.cloned.1.call-start = ((), (), s32[]{:S(2)}) async-start(), calls=%async_computation.3 | async-start | bytes 7340032 | tf_op jit(solution)/shard_map/psum | solution.py:30
  413.9 312.9 %all-gather.10.cloned.1.call-start = ((), (), s32[]{:S(2)}) async-start(), calls=%async_computation.5 | async-start | bytes 22020096 | tf_op jit(solution)/shard_map/all_gather | solution.py:40
  553.8 7.9 %copy-start = (bf16[3584,512]{1,0:T(8,128)(2,1)S(1)}, bf16[3584,512]{1,0:T(8,128)(2,1)}, u32[]{:S(2)}) copy-start(bf16[3584,512]{1,0:T(8,128)(2,1)} %all-reduce.3.cloned.1.call-done) | copy-start | bytes 11010052
Sparse Core Ops, SparseCore 0:
  36.6 46.3 reduce-scatter.1
  86.3 125.6 all-gather.7
  213.6 43.9 all-gather.5
  414.0 75.1 all-reduce.2
  553.9 172.8 all-gather.9
